TPU v7x, 1024 devices: a whole 4x4x32 slice. The times are simulated.
1024 devices in a mesh: sp: 32 (over y, x, core), dp: 32 (over z).
Axes of the slice: x: 4, y: 4, z: 32, core: 2. Of those that a mesh axis runs over, the one named last changes fastest.
Arguments:
- hidden: bfloat16 [32, 8192, 4096], P('dp', 'sp'), may hold values from -24 to 24
- pad_counts: int32 [32, 32], P('dp', 'sp'), may hold values from 64 to 128
- doc_lengths: int32 [32, 128], P('dp'), may hold values from 1 to 128, 8192 in all within a row
- range_shift: int32 [32, 32], P('dp'), may hold values from -32 to 32
- qkv_weight: bfloat16 [4096, 384], P('dp'), may hold values from -0.09375 to 0.09375
Outputs:
- attended: bfloat16 [32, 8192, 128], P('dp', 'sp')
Inputs may be any that keep to these rules, and one draw needn't show every extreme that they name: `doc_lengths`: each row sums to 8192.
All inputs are finite; a program needn't handle non-finite values.
Results may differ from a plain program's by a relative error of at most 0.0095.
Values may be sent and summed in bfloat16 or wider, within the bound.
No kernel may reach another device: no remote copies, remote signals or barrier semaphores. Data moves between devices by JAX's collectives and lax.ppermute only.
A program may use at most 32 MiB of HBM per device.

v0:
```python
import math

import jax
import jax.numpy as jnp
from jax import lax
from jax.sharding import PartitionSpec as P


def copy_for_each(value, axis):
    devices = lax.axis_size(axis)
    return lax.all_to_all(
        jnp.broadcast_to(value[None], (devices, *value.shape)), axis, 0, 0, tiled=True
    )


def combined_pairwise(pieces, combine):
    while len(jax.tree.leaves(pieces)[0]) > 1:
        pieces = jax.vmap(combine)(*(pieces[side::2] for side in (0, 1)))
    return pieces[0]


def prefix(value, axis, combine, identity):
    devices, index = (lax.axis_size(axis), lax.axis_index(axis))
    passed = jnp.arange(devices) < index

    def kept(part, zero, own):
        part = jnp.where(
            passed.reshape(-1, *(1 for _ in own.shape)), part, jnp.asarray(zero, own.dtype)
        )
        return part

    pieces = copy_for_each(value, axis)
    return combined_pairwise(kept(pieces, identity, value), combine)


def extended_2(cells, sides, width):
    for axis, dim in sides:
        count = lax.axis_size(axis)
        ends = count - 1
        head = lax.slice_in_dim(cells, 0, width, axis=dim)
        tail = lax.slice_in_dim(cells, cells.shape[dim] - width, cells.shape[dim], axis=dim)
        cells = jnp.concatenate(
            [
                lax.ppermute(tail, axis, [(i, (i + 1) % count) for i in range(ends)]),
                cells,
                lax.ppermute(head, axis, [((i + 1) % count, i) for i in range(ends)]),
            ],
            axis=dim,
        )
    return cells


def add_counts(earlier, later):
    return earlier + later


def edge_slots(rows, padding, edge_count):
    total_rows = rows.shape[0]
    return jnp.concatenate(
        [lax.dynamic_slice_in_dim(rows, padding, edge_count, 0), rows[total_rows - edge_count :]],
        axis=0,
    )


def with_edges(rows, extended, edge_count):
    return jnp.concatenate([extended[:edge_count], rows, extended[3 * edge_count :]], axis=0)


def project(inputs, qkv_weight):
    summed = jnp.dot(
        inputs,
        lax.all_gather(qkv_weight, "dp", axis=0, tiled=True),
        preferred_element_type=jnp.float32,
    )
    return summed.astype(jnp.bfloat16)


def shards(hidden, pad_counts, doc_lengths, range_shift, qkv_weight):
    slot_rows = hidden[0]
    rows_dev = slot_rows.shape[0]
    edge_count = rows_dev // 8
    padding = pad_counts[0, 0]
    live_count = rows_dev - padding
    token_start = prefix(live_count, "sp", add_counts, jnp.int32(0))
    axis_size = lax.axis_size("sp")
    device_index = lax.axis_index("sp")
    shifts = range_shift[0]
    range_first = jnp.where(
        device_index == 0, 0, token_start + jnp.take(shifts, device_index)
    ).astype(jnp.int32)
    next_shift = jnp.take(shifts, jnp.minimum(device_index + 1, axis_size - 1))
    range_end = jnp.where(
        device_index == axis_size - 1,
        token_start + live_count,
        token_start + live_count + next_shift,
    ).astype(jnp.int32)
    owned_count = range_end - range_first
    local_rows = jnp.arange(rows_dev, dtype=jnp.int32)
    position = range_first + local_rows
    row_live = local_rows < owned_count
    source = position - token_start + edge_count + jnp.where(position >= token_start, padding, 0)
    source = jnp.clip(source, 0, rows_dev + 2 * edge_count - 1)
    extended = extended_2(edge_slots(slot_rows, padding, edge_count), (("sp", 0),), edge_count)
    candidates = with_edges(slot_rows, extended, edge_count)
    owned_rows = jnp.where(row_live[:, None], jnp.take(candidates, source, axis=0), 0)
    projected = project(owned_rows, qkv_weight)
    head_dim = projected.shape[1] // 3
    query = projected[:, :head_dim]
    keys = projected[:, head_dim : 2 * head_dim]
    values = projected[:, 2 * head_dim :]
    doc_ends = jnp.cumsum(doc_lengths[0])
    doc_ids = jnp.sum((doc_ends[None, :] <= position[:, None]).astype(jnp.int32), axis=1)
    scores = jnp.einsum("qd,kd->qk", query, keys, preferred_element_type=jnp.float32) / math.sqrt(
        head_dim
    )
    allowed = (doc_ids[:, None] == doc_ids[None, :]) & (position[None, :] <= position[:, None])
    allowed = allowed & row_live[:, None] & row_live[None, :]
    masked = jnp.where(allowed, scores, -1e30)
    row_peak = jnp.max(masked, axis=1, keepdims=True)
    exponent = jnp.where(allowed, jnp.exp(masked - row_peak), 0.0)
    denominator = jnp.sum(exponent, axis=1, keepdims=True)
    attention_probs = (exponent / jnp.where(row_live[:, None], denominator, 1.0)).astype(
        jnp.bfloat16
    )
    result = jnp.dot(attention_probs, values, preferred_element_type=jnp.float32)
    attended = jnp.where(row_live[:, None], result, 0.0).astype(jnp.bfloat16)
    return attended[None]


def solution(mesh):
    in_specs = (P("dp", "sp", None), P("dp", "sp"), P("dp", None), P("dp", None), P("dp", None))
    out_specs = P("dp", "sp", None)
    return jax.shard_map(shards, mesh=mesh, in_specs=in_specs, out_specs=out_specs, check_vma=False)
```

profile of v0, /device:TPU:2, one launch (start us, length us, event | category | flops | bytes accessed | tf_op | source)
XLA Modules:
  0.0 170.4 jit_solution(11429874976681333694)
XLA Ops:
  6.5 0.0 all-gather.2.cloned.1.call-start
  6.5 0.7 all-gather.2.cloned.1.call-update
  7.9 0.6 broadcast_in_dim.86
  8.5 16.6 %all-to-all-start = ((s32[32,1,1]{2,1,0:T(1,128)}), s32[32,1,1]{2,1,0:T(1,128)S(1)}, u32[]{:S(2)}, u32[]{:S(2)}) async-start(s32[32,1,1]{2,1,0:T(1,128)} %broadcast_in_dim.86), calls=%async_computation | async-start | bytes 32768 | tf_op jit(solution)/shard_map/all_to_all | solution.py:11
  25.2 1.1 slice_bitcast_fusion
  26.3 2.0 %collective-permute-start = (bf16[32,4096]{1,0:T(8,128)(2,1)S(1)}, bf16[32,4096]{1,0:T(8,128)(2,1)S(1)}, u32[]{:S(2)}, u32[]{:S(2)}) collective-permute-start(bf16[32,4096]{1,0:T(8,128)(2,1)S(1)} %get-tuple-element.27), channel_id=1, source_target_pairs={{0,32},{32,64},{64,96},{96,128},{128,160},{160,192},{192,224},{224... | collective-permute-start | bytes 786440 | tf_op jit(solution)/shard_map/ppermute | solution.py:44
  28.3 3.5 %collective-permute-start.1 = (bf16[32,4096]{1,0:T(8,128)(2,1)S(1)}, bf16[32,4096]{1,0:T(8,128)(2,1)S(1)}, u32[]{:S(2)}, u32[]{:S(2)}) collective-permute-start(bf16[32,4096]{1,0:T(8,128)(2,1)S(1)} %get-tuple-element.28), channel_id=1, source_target_pairs={{32,0},{64,32},{96,64},{128,96},{160,128},{192,160},{224,192},{256... | collective-permute-start | bytes 786440 | tf_op jit(solution)/shard_map/ppermute | solution.py:46
  31.9 0.8 copy.10
  32.7 0.2 reduce-window.8
  32.8 0.1 reduce.1
  32.9 1.4 constant_dynamic-slice_fusion.1
  35.6 0.0 all-to-all-done
  35.6 0.7 reduce
  36.3 0.1 slice.47
  36.4 0.1 slice.48
  36.5 0.1 slice.49
  36.6 0.1 slice.50
  36.7 0.1 slice.51
  36.8 0.1 slice.52
  36.9 0.1 slice.53
  37.0 0.1 slice.54
  37.1 0.6 fusion.23
  39.1 0.2 convert_reduce_fusion
  39.3 0.0 collective-permute-done
  39.3 0.0 collective-permute-done.1
  39.3 1.8 %pad_maximum_fusion = bf16[320,4096]{1,0:T(8,128)(2,1)S(1)} fusion(bf16[32,4096]{1,0:T(8,128)(2,1)S(1)} %collective-permute-done.1, bf16[256,4096]{1,0:T(8,128)(2,1)} %bitcast.24, bf16[32,4096]{1,0:T(8,128)(2,1)S(1)} %collective-permute-done), kind=kLoop, calls=%fused_computation.1 | loop fusion | flops 7864320 | bytes 5242880 | tf_op jit(solution)/shard_map/concatenate | solution.py:66
  41.1 3.2 %gather_fusion = bf16[256,4096]{1,0:T(8,128)(2,1)} fusion(bf16[320,4096]{1,0:T(8,128)(2,1)S(1)} %pad_maximum_fusion, s32[1024]{0:T(1024)S(1)} %pad_clamp_fusion), kind=kCustom, calls=%fused_computation | custom fusion | bytes 4195328 | tf_op jit(solution)/shard_map/jit(_take)/gather | solution.py:105
  44.3 114.0 %all-gather.2.cloned.1.call-done = bf16[4096,384]{1,0:T(8,128)(2,1)} async-done(((bf16[128,384]{1,0:T(8,128)(2,1)}), bf16[4096,384]{1,0:T(8,128)(2,1)}) %all-gather.2.cloned.1.call-update) | async-done | bytes 3145744 | tf_op jit(solution)/shard_map/all_gather | solution.py:72
  158.3 3.8 %fusion.5 = bf16[256,384]{1,0:T(8,128)(2,1)S(1)} fusion(bf16[4096,384]{1,0:T(8,128)(2,1)} %all-gather.2.cloned.1.call-done, bf16[256,4096]{1,0:T(8,128)(2,1)} %gather_fusion, pred[256]{0:T(512)(128)(4,1)S(1)} %get-tuple-element.35, pred[256]{0:T(512)(128)(4,1)S(1)} %get-tuple-element.36), kind=kOutput, calls=%fused_computation.7 | convolution fusion | flops 807501824 | bytes 5440000 | tf_op jit(solution)/shard_map/dot_general | solution.py:70
  162.1 0.2 fusion.24
  162.4 0.2 fusion.13
  162.6 1.0 fusion.10
  (10 shorter events, 0.1 us)
Async XLA Ops:
  6.5 151.8 %all-gather.2.cloned.1.call-start = ((), (), s32[]{:S(2)}) async-start(), calls=%async_computation.1 | async-start | bytes 3244032 | tf_op jit(solution)/shard_map/all_gather | solution.py:72
  8.5 27.1 %all-to-all-start = ((s32[32,1,1]{2,1,0:T(1,128)}), s32[32,1,1]{2,1,0:T(1,128)S(1)}, u32[]{:S(2)}, u32[]{:S(2)}) async-start(s32[32,1,1]{2,1,0:T(1,128)} %broadcast_in_dim.86), calls=%async_computation | async-start | bytes 32768 | tf_op jit(solution)/shard_map/all_to_all | solution.py:11
  26.3 13.0 %collective-permute-start = (bf16[32,4096]{1,0:T(8,128)(2,1)S(1)}, bf16[32,4096]{1,0:T(8,128)(2,1)S(1)}, u32[]{:S(2)}, u32[]{:S(2)}) collective-permute-start(bf16[32,4096]{1,0:T(8,128)(2,1)S(1)} %get-tuple-element.27), channel_id=1, source_target_pairs={{0,32},{32,64},{64,96},{96,128},{128,160},{160,192},{192,224},{224... | collective-permute-start | bytes 786440 | tf_op jit(solution)/shard_map/ppermute | solution.py:44
  28.3 11.0 %collective-permute-start.1 = (bf16[32,4096]{1,0:T(8,128)(2,1)S(1)}, bf16[32,4096]{1,0:T(8,128)(2,1)S(1)}, u32[]{:S(2)}, u32[]{:S(2)}) collective-permute-start(bf16[32,4096]{1,0:T(8,128)(2,1)S(1)} %get-tuple-element.28), channel_id=1, source_target_pairs={{32,0},{64,32},{96,64},{128,96},{160,128},{192,160},{224,192},{256... | collective-permute-start | bytes 786440 | tf_op jit(solution)/shard_map/ppermute | solution.py:46
Sparse Core Ops, SparseCore 0:
  10.0 148.2 all-gather.1
where the time goes:
time: 171 us; the launch traced here: 170 us
  waiting for transfers between devices  115 us (67%)
  starting transfers between devices  22.2 us (13%)
  between operations  16.8 us (10%)
  local copies, waits for them, and re-layouts  8.51 us (5%)
  matrix products  5.07 us (3%)
  other arithmetic  3.14 us (2%)
    all_gather x1, waiting for transfers between devices, project(): lax.all_gather(qkv_weight, 'dp', axis=0, tiled=True)  114 us
    all_to_all x1, starting transfers between devices, copy_for_each(): lax.all_to_all(jnp.broadcast_to(value[None], (devices, *value.shape)), ax...  16.6 us
    dot_general x1, matrix products, project(): jnp.dot(inputs, lax.all_gather(qkv_weight, 'dp', axis=0, tiled=True), pre...  3.83 us
    ppermute x1, starting transfers between devices, extended_2(): lax.ppermute(head, axis, [((i + 1) % count, i) for i in range(ends)])  3.53 us
  transfers between devices with their start and end apart: 4, of which 1 were waited for; matrix products, arithmetic and copies ran while one was open for 7% of the time, Pallas kernels for 0%

commit v1 on v0

v1 whole, which is shorter than its diff:
```python
import functools
import math

import jax
import jax.numpy as jnp
from jax import lax
from jax.experimental import pallas as pl
from jax.experimental.pallas import tpu as pltpu
from jax.sharding import Mesh
from jax.sharding import PartitionSpec as P

PLANE = ("y", "x", "core")
EDGE = 32
CHUNK = 512
SMALL = pltpu.CompilerParams(vmem_limit_bytes=16 * 1024 * 1024)


def gather_kernel(scalars, slots, left, right, owned):
    rows = slots.shape[0]
    padding, live, shift, count = (scalars[i] for i in range(4))
    row = lax.broadcasted_iota(jnp.int32, (rows, 1), 0)
    offset = row + shift
    slot = jnp.where(
        offset < 0,
        rows + EDGE + offset,
        jnp.where(offset < live, padding + offset, rows + EDGE + offset - live),
    )
    slot = jnp.where(row < count, slot, -1)
    here = lax.broadcasted_iota(jnp.int32, (rows, rows), 1)
    edge = lax.broadcasted_iota(jnp.int32, (rows, 2 * EDGE), 1) + rows
    pick_here = jnp.where(here == slot, 1.0, 0.0).astype(jnp.bfloat16)
    pick_edge = jnp.where(edge == slot, 1.0, 0.0).astype(jnp.bfloat16)
    for at in range(0, slots.shape[1], CHUNK):
        columns = slice(at, at + CHUNK)
        edges = jnp.concatenate([left[:, columns], right[:, columns]], axis=0)
        owned[:, columns] = (
            jnp.dot(pick_here, slots[:, columns], preferred_element_type=jnp.float32)
            + jnp.dot(pick_edge, edges, preferred_element_type=jnp.float32)
        ).astype(jnp.bfloat16)


def gather_rows(scalars, slots, left, right):
    rows, width = slots.shape
    return pl.pallas_call(
        gather_kernel,
        out_shape=jax.ShapeDtypeStruct((rows, width), jnp.bfloat16),
        in_specs=[pl.BlockSpec(memory_space=pltpu.SMEM)]
        + [pl.BlockSpec(memory_space=pltpu.VMEM)] * 3,
        out_specs=pl.BlockSpec(memory_space=pltpu.VMEM),
        cost_estimate=pl.CostEstimate(
            flops=2 * rows * (rows + 2 * EDGE) * width,
            bytes_accessed=4 * rows * width,
            transcendentals=0,
        ),
        compiler_params=SMALL,
        name="gather_rows",
    )(scalars, slots, left, right)


def weave_kernel(core, half, other, weight):
    chips, heads, parts = half.shape[:3]

    def one(part, carry):
        for at in range(chips):
            for head in range(heads):
                weight[head, part, 2 * at + core[0]] = half[at, head, part]
                weight[head, part, 2 * at + 1 - core[0]] = other[at, head, part]
        return carry

    lax.fori_loop(0, parts, one, 0)


def weave(core, half, other):
    chips, heads, parts, deep, lanes = half.shape
    return pl.pallas_call(
        weave_kernel,
        out_shape=jax.ShapeDtypeStruct((heads, parts, 2 * chips, deep, lanes), jnp.bfloat16),
        in_specs=[pl.BlockSpec(memory_space=pltpu.SMEM)]
        + [pl.BlockSpec(memory_space=pltpu.VMEM)] * 2,
        out_specs=pl.BlockSpec(memory_space=pltpu.VMEM),
        compiler_params=SMALL,
        name="weave",
    )(core, half, other)


def attend_kernel(scalars, owned, weight, ends, attended):
    rows = owned.shape[0]
    head_dim = attended.shape[1]
    start, count = scalars[0], scalars[1]
    pair = jnp.concatenate([weight[0], weight[1]], axis=1)
    both = jnp.dot(owned[...], pair, preferred_element_type=jnp.float32).astype(jnp.bfloat16)
    values = jnp.dot(owned[...], weight[2], preferred_element_type=jnp.float32).astype(
        jnp.bfloat16
    )
    query, keys = both[:, :head_dim], both[:, head_dim:]
    scores = lax.dot_general(
        query, keys, (((1,), (1,)), ((), ())), preferred_element_type=jnp.float32
    ) / math.sqrt(head_dim)
    row = lax.broadcasted_iota(jnp.int32, (rows, 1), 0)
    key = lax.broadcasted_iota(jnp.int32, (rows, rows), 1)
    passed = jnp.where(ends[...] <= row + start, ends[...], 0)
    opened = jnp.max(passed, axis=1, keepdims=True) - start
    live = row < count
    allowed = (key <= row) & (key >= opened) & live
    masked = jnp.where(allowed, scores, -1e30)
    peak = jnp.max(masked, axis=1, keepdims=True)
    exponent = jnp.where(allowed, jnp.exp(masked - peak), 0.0)
    denominator = jnp.sum(exponent, axis=1, keepdims=True)
    probs = (exponent / jnp.where(live, denominator, 1.0)).astype(jnp.bfloat16)
    result = jnp.dot(probs, values, preferred_element_type=jnp.float32)
    attended[...] = jnp.where(live, result, 0.0).astype(jnp.bfloat16)


def attend(scalars, owned, weight, ends):
    rows, head_dim = owned.shape[0], weight.shape[2]
    return pl.pallas_call(
        attend_kernel,
        out_shape=jax.ShapeDtypeStruct((rows, head_dim), jnp.bfloat16),
        in_specs=[pl.BlockSpec(memory_space=pltpu.SMEM)]
        + [pl.BlockSpec(memory_space=pltpu.VMEM)] * 3,
        out_specs=pl.BlockSpec(memory_space=pltpu.VMEM),
        compiler_params=SMALL,
        name="attend",
    )(scalars, owned, weight, ends)


def for_each(value, count):
    return jnp.broadcast_to(value[None], (count, *value.shape))


def weight_column(own):
    index = lax.axis_index(PLANE)
    deep = own.shape[0] // lax.axis_size(PLANE)
    lanes = own.shape[1] // 3
    piece = lax.dynamic_slice_in_dim(own, index * deep, deep, 0)
    piece = piece.reshape(deep, 3, lanes).transpose(1, 0, 2)
    column = lax.all_to_all(for_each(piece, lax.axis_size("z")), "z", 0, 0, tiled=True)
    return column.transpose(1, 0, 2, 3)


def shards(hidden, pad_counts, doc_lengths, range_shift, qkv_weight):
    slots = hidden[0]
    rows = slots.shape[0]
    size, index = lax.axis_size(PLANE), lax.axis_index(PLANE)
    padding = pad_counts[0, 0]
    live = rows - padding

    column = weight_column(qkv_weight)

    head = lax.dynamic_slice_in_dim(slots, padding, EDGE, 0)
    tail = slots[rows - EDGE :]
    left = lax.ppermute(tail, PLANE, [(i, i + 1) for i in range(size - 1)])
    right = lax.ppermute(head, PLANE, [(i + 1, i) for i in range(size - 1)])
    counts = lax.all_to_all(
        jnp.broadcast_to(live, (size, 1)), PLANE, 0, 0, tiled=True
    )[:, 0]
    column, counts = lax.optimization_barrier((column, counts))

    chips = lax.axis_size(("y", "x"))
    half = lax.all_to_all(for_each(column, chips), ("y", "x"), 0, 0, tiled=True)

    token_start = jnp.sum(jnp.where(jnp.arange(size) < index, counts, 0))
    shifts = range_shift[0]
    shift = jnp.where(index == 0, 0, shifts[index])
    following = jnp.where(index == size - 1, 0, shifts[jnp.minimum(index + 1, size - 1)])
    count = live + following - shift
    scalars = jnp.stack([padding, live, shift, count]).astype(jnp.int32)
    owned = gather_rows(scalars, slots, left, right)
    ends = jnp.cumsum(doc_lengths[0])[None]
    where = jnp.stack([token_start + shift, count]).astype(jnp.int32)
    half, owned, ends, where = lax.optimization_barrier((half, owned, ends, where))

    other = lax.ppermute(half, "core", [(0, 1), (1, 0)])
    core = lax.axis_index("core").reshape(1)
    weight = weave(core, half, other)
    weight = weight.reshape(3, -1, weight.shape[-1])
    return attend(where, owned, weight, ends)[None]


def solution(mesh):
    fine = Mesh(mesh.devices.reshape(4, 4, 2, -1), ("y", "x", "core", "z"))
    in_specs = (P("z", PLANE, None), P("z", PLANE), P("z", None), P("z", None), P("z", None))
    return jax.shard_map(
        shards, mesh=fine, in_specs=in_specs, out_specs=P("z", PLANE, None), check_vma=False
    )
```

time: 171 us -> 118 us (0.69)
  the two profiles are of different devices: /device:TPU:2 before, /device:TPU:1 now
where the time goes in v1:
time: 118 us
  starting transfers between devices  51.5 us (44%)
  waiting for transfers between devices  47.5 us (40%)
  Pallas kernels  7.89 us (7%)
  local copies, waits for them, and re-layouts  6.61 us (6%)
  between operations  2.69 us (2%)
  other arithmetic  1.76 us (1%)
    all_to_all x1, waiting for transfers between devices, weight_column(): lax.all_to_all(for_each(piece, lax.axis_size('z')), 'z', 0, 0, tiled=True)  26 us
    all_to_all x1, starting transfers between devices, weight_column(): lax.all_to_all(for_each(piece, lax.axis_size('z')), 'z', 0, 0, tiled=True)  19.3 us
    all_to_all x1, starting transfers between devices, shards(): lax.all_to_all(jnp.broadcast_to(live, (size, 1)), PLANE, 0, 0, tiled=True)  17.6 us
    ppermute x1, waiting for transfers between devices, shards(): right = lax.ppermute(head, PLANE, [(i + 1, i) for i in range(size - 1)])  11 us
    all_to_all x1, waiting for transfers between devices, shards(): lax.all_to_all(jnp.broadcast_to(live, (size, 1)), PLANE, 0, 0, tiled=True)  6.96 us
    ppermute x1, starting transfers between devices, shards(): right = lax.ppermute(head, PLANE, [(i + 1, i) for i in range(size - 1)])  4.91 us
    all_to_all x1, starting transfers between devices, shards(): half = lax.all_to_all(for_each(column, chips), ('y', 'x'), 0, 0, tiled=True)  4.54 us
    ppermute x1, waiting for transfers between devices, shards(): other = lax.ppermute(half, 'core', [(0, 1), (1, 0)])  3.59 us
  transfers between devices with their start and end apart: 6, of which 4 were waited for; matrix products, arithmetic and copies ran while one was open for 3% of the time, Pallas kernels for 2%

profile of v1, /device:TPU:1, one launch (start us, length us, event | category | flops | bytes accessed | tf_op | source)
XLA Modules:
  0.0 118.0 jit_solution(6391508850355393856)
XLA Ops:
  0.0 0.0 copy-start
  0.7 0.6 broadcast_in_dim.24
  1.3 17.6 %all-to-all-start.1 = ((s32[32,1,1]{2,1,0:T(1,128)}), s32[32,1,1]{2,1,0:T(1,128)S(1)}, u32[]{:S(2)}, u32[]{:S(2)}) async-start(s32[32,1,1]{2,1,0:T(1,128)} %broadcast_in_dim.24), calls=%async_computation.1 | async-start | bytes 32768 | tf_op jit(solution)/shard_map/all_to_all | solution.py:154
  18.9 0.0 copy-done
  19.0 7.0 %all-to-all-done.1 = s32[32,1,1]{2,1,0:T(1,128)S(1)} async-done(((s32[32,1,1]{2,1,0:T(1,128)}), s32[32,1,1]{2,1,0:T(1,128)S(1)}, u32[]{:S(2)}, u32[]{:S(2)}) %all-to-all-start.1) | async-done | bytes 160 | tf_op jit(solution)/shard_map/all_to_all | solution.py:154
  25.9 0.7 broadcast_in_dim.12
  26.6 19.3 %all-to-all-start = ((bf16[32,3,4,128]{3,2,1,0:T(4,128)(2,1)}), bf16[32,3,4,128]{3,2,1,0:T(4,128)(2,1)S(1)}, u32[]{:S(2)}, u32[]{:S(2)}) async-start(bf16[32,3,4,128]{3,2,1,0:T(4,128)(2,1)} %broadcast_in_dim.12), calls=%async_computation | async-start | bytes 196608 | tf_op jit(solution)/shard_map/all_to_all | solution.py:137
  45.9 0.7 reduce
  46.6 26.0 %all-to-all-done = bf16[32,3,4,128]{3,2,1,0:T(4,128)(2,1)S(1)} async-done(((bf16[32,3,4,128]{3,2,1,0:T(4,128)(2,1)}), bf16[32,3,4,128]{3,2,1,0:T(4,128)(2,1)S(1)}, u32[]{:S(2)}, u32[]{:S(2)}) %all-to-all-start) | async-done | bytes 98336 | tf_op jit(solution)/shard_map/all_to_all | solution.py:137
  72.6 1.9 %broadcast_in_dim.25 = bf16[16,3,32,4,128]{4,3,2,1,0:T(4,128)(2,1)} broadcast(bf16[3,32,4,128]{3,2,1,0:T(4,128)(2,1)S(1)} %copy.7), dimensions={1,2,3,4} | broadcast | bytes 1671168 | tf_op jit(solution)/shard_map/broadcast_in_dim | solution.py:128
  74.5 0.0 copy-start.2
  74.5 0.0 copy-start.3
  74.5 4.5 %all-to-all-start.2 = ((bf16[16,3,32,4,128]{4,3,2,1,0:T(4,128)(2,1)}), bf16[16,3,32,4,128]{4,3,2,1,0:T(4,128)(2,1)}, u32[]{:S(2)}, u32[]{:S(2)}) async-start(bf16[16,3,32,4,128]{4,3,2,1,0:T(4,128)(2,1)} %broadcast_in_dim.25), calls=%async_computation.2 | async-start | bytes 3145728 | tf_op jit(solution)/shard_map/all_to_all | solution.py:160
  79.0 1.1 dynamic-slice_bitcast_fusion
  80.2 4.9 %collective-permute-start.1 = (bf16[32,4096]{1,0:T(8,128)(2,1)S(1)}, bf16[32,4096]{1,0:T(8,128)(2,1)S(1)}, u32[]{:S(2)}, u32[]{:S(2)}) collective-permute-start(bf16[32,4096]{1,0:T(8,128)(2,1)S(1)} %get-tuple-element.17), channel_id=1, source_target_pairs={{32,0},{64,32},{96,64},{128,96},{160,128},{192,160},{224,192},{256... | collective-permute-start | bytes 786440 | tf_op jit(solution)/shard_map/ppermute | solution.py:153
  85.1 3.3 %collective-permute-start = (bf16[32,4096]{1,0:T(8,128)(2,1)S(1)}, bf16[32,4096]{1,0:T(8,128)(2,1)S(1)}, u32[]{:S(2)}, u32[]{:S(2)}) collective-permute-start(bf16[32,4096]{1,0:T(8,128)(2,1)S(1)} %get-tuple-element.18), channel_id=1, source_target_pairs={{0,32},{32,64},{64,96},{96,128},{128,160},{160,192},{192,224},{224... | collective-permute-start | bytes 786440 | tf_op jit(solution)/shard_map/ppermute | solution.py:152
  88.4 0.0 copy-done.2
  88.4 0.6 constant_dynamic-slice_fusion.1
  89.6 0.0 copy-done.3
  89.7 0.3 reduce-window_clone.1.ends
  90.6 0.1 pad_add_fusion.scalars
  90.7 11.0 %collective-permute-done.1.right = bf16[32,4096]{1,0:T(8,128)(2,1)S(1)} collective-permute-done((bf16[32,4096]{1,0:T(8,128)(2,1)S(1)}, bf16[32,4096]{1,0:T(8,128)(2,1)S(1)}, u32[]{:S(2)}, u32[]{:S(2)}) %collective-permute-start.1) | collective-permute-done | bytes 262176 | tf_op jit(solution)/shard_map/ppermute | solution.py:153
  101.7 0.0 collective-permute-done.left
  101.7 1.6 %copy-done.1 = bf16[1,256,4096]{2,1,0:T(8,128)(2,1)S(1)} copy-done((bf16[1,256,4096]{2,1,0:T(8,128)(2,1)S(1)}, bf16[1,256,4096]{2,1,0:T(8,128)(2,1)}, u32[]{:S(2)}) %copy-start.1) | copy-done | bytes 2097176
  103.3 1.8 %gather_rows.1.owned = bf16[256,4096]{1,0:T(8,128)(2,1)S(1)} custom-call(s32[4]{0:T(128)S(1)} %pad_add_fusion.scalars, bf16[256,4096]{1,0:T(8,128)(2,1)S(1)} %bitcast.27, bf16[32,4096]{1,0:T(8,128)(2,1)S(1)} %collective-permute-done.left, bf16[32,4096]{1,0:T(8,128)(2,1)S(1)} %collective-permute-done.1.right), custom_call_target="tpu_custom_call" | custom-call | flops 671088640 | bytes 4194304 | tf_op jit(solution)/shard_map/gather_rows/pallas_call | solution.py:44
  105.0 0.6 fusion
  106.2 0.1 pad_add_fusion.1.scalars
  106.3 0.0 all-to-all-done.2.half
  106.3 1.9 %collective-permute-start.2 = (bf16[16,3,32,4,128]{4,3,2,1,0:T(4,128)(2,1)}, bf16[16,3,32,4,128]{4,3,2,1,0:T(4,128)(2,1)S(1)}, u32[]{:S(2)}, u32[]{:S(2)}) collective-permute-start(bf16[16,3,32,4,128]{4,3,2,1,0:T(4,128)(2,1)} %all-to-all-done.2.half), channel_id=1, source_target_pairs={{0,32},{32,0},{1,33},{33,1},{2,34},{34,2},{3,35},{35,3},{4,36},{36... | collective-permute-start | bytes 4718600 | tf_op jit(solution)/shard_map/ppermute | solution.py:173
  108.2 3.6 %collective-permute-done.2.other = bf16[16,3,32,4,128]{4,3,2,1,0:T(4,128)(2,1)S(1)} collective-permute-done((bf16[16,3,32,4,128]{4,3,2,1,0:T(4,128)(2,1)}, bf16[16,3,32,4,128]{4,3,2,1,0:T(4,128)(2,1)S(1)}, u32[]{:S(2)}, u32[]{:S(2)}) %collective-permute-start.2) | collective-permute-done | bytes 1572896 | tf_op jit(solution)/shard_map/ppermute | solution.py:173
  111.8 3.2 %weave.1 = bf16[3,32,32,4,128]{4,3,2,1,0:T(4,128)(2,1)S(1)} custom-call(s32[1]{0:T(128)} %bitcast.14.core, bf16[16,3,32,4,128]{4,3,2,1,0:T(4,128)(2,1)} %all-to-all-done.2.half, bf16[16,3,32,4,128]{4,3,2,1,0:T(4,128)(2,1)S(1)} %collective-permute-done.2.other), custom_call_target="tpu_custom_call" | custom-call | tf_op jit(solution)/shard_map/weave/pallas_call | solution.py:75
  115.0 2.9 %attend.1 = bf16[256,128]{1,0:T(8,128)(2,1)} custom-call(s32[2]{0:T(128)S(1)} %pad_add_fusion.1.scalars, bf16[256,4096]{1,0:T(8,128)(2,1)S(1)} %gather_rows.1.owned, bf16[3,4096,128]{2,1,0:T(8,128)(2,1)S(1)} %bitcast.26, s32[1,128]{1,0:T(1,128)S(1)} %reduce-window_clone.1.ends), custom_call_target="tpu_custom_call" | custom-call | tf_op jit(solution)/shard_map/attend/pallas_call | solution.py:116
  (3 shorter events, 0.1 us)
Async XLA Ops:
  0.0 18.9 %copy-start = (bf16[128,384]{1,0:T(8,128)(2,1)S(1)}, bf16[128,384]{1,0:T(8,128)(2,1)}, u32[]{:S(2)}) copy-start(bf16[128,384]{1,0:T(8,128)(2,1)} %param.9) | copy-start | bytes 294916
  1.3 24.6 %all-to-all-start.1 = ((s32[32,1,1]{2,1,0:T(1,128)}), s32[32,1,1]{2,1,0:T(1,128)S(1)}, u32[]{:S(2)}, u32[]{:S(2)}) async-start(s32[32,1,1]{2,1,0:T(1,128)} %broadcast_in_dim.24), calls=%async_computation.1 | async-start | bytes 32768 | tf_op jit(solution)/shard_map/all_to_all | solution.py:154
  26.6 45.9 %all-to-all-start = ((bf16[32,3,4,128]{3,2,1,0:T(4,128)(2,1)}), bf16[32,3,4,128]{3,2,1,0:T(4,128)(2,1)S(1)}, u32[]{:S(2)}, u32[]{:S(2)}) async-start(bf16[32,3,4,128]{3,2,1,0:T(4,128)(2,1)} %broadcast_in_dim.12), calls=%async_computation | async-start | bytes 196608 | tf_op jit(solution)/shard_map/all_to_all | solution.py:137
  74.5 13.9 %copy-start.2 = (s32[1,32]{1,0:T(1,128)S(1)}, s32[1,32]{1,0:T(1,128)}, u32[]{:S(2)}) copy-start(s32[1,32]{1,0:T(1,128)} %param.8) | copy-start | bytes 388
  74.5 15.2 %copy-start.3 = (s32[1,128]{1,0:T(1,128)S(1)}, s32[1,128]{1,0:T(1,128)}, u32[]{:S(2)}) copy-start(s32[1,128]{1,0:T(1,128)} %param.7) | copy-start | bytes 1540
  74.5 31.8 %all-to-all-start.2 = ((bf16[16,3,32,4,128]{4,3,2,1,0:T(4,128)(2,1)}), bf16[16,3,32,4,128]{4,3,2,1,0:T(4,128)(2,1)}, u32[]{:S(2)}, u32[]{:S(2)}) async-start(bf16[16,3,32,4,128]{4,3,2,1,0:T(4,128)(2,1)} %broadcast_in_dim.25), calls=%async_computation.2 | async-start | bytes 3145728 | tf_op jit(solution)/shard_map/all_to_all | solution.py:160
  80.2 21.5 %collective-permute-start.1 = (bf16[32,4096]{1,0:T(8,128)(2,1)S(1)}, bf16[32,4096]{1,0:T(8,128)(2,1)S(1)}, u32[]{:S(2)}, u32[]{:S(2)}) collective-permute-start(bf16[32,4096]{1,0:T(8,128)(2,1)S(1)} %get-tuple-element.17), channel_id=1, source_target_pairs={{32,0},{64,32},{96,64},{128,96},{160,128},{192,160},{224,192},{256... | collective-permute-start | bytes 786440 | tf_op jit(solution)/shard_map/ppermute | solution.py:153
  85.1 16.6 %collective-permute-start = (bf16[32,4096]{1,0:T(8,128)(2,1)S(1)}, bf16[32,4096]{1,0:T(8,128)(2,1)S(1)}, u32[]{:S(2)}, u32[]{:S(2)}) collective-permute-start(bf16[32,4096]{1,0:T(8,128)(2,1)S(1)} %get-tuple-element.18), channel_id=1, source_target_pairs={{0,32},{32,64},{64,96},{96,128},{128,160},{160,192},{192,224},{224... | collective-permute-start | bytes 786440 | tf_op jit(solution)/shard_map/ppermute | solution.py:152
  101.7 1.6 %copy-start.1 = (bf16[1,256,4096]{2,1,0:T(8,128)(2,1)S(1)}, bf16[1,256,4096]{2,1,0:T(8,128)(2,1)}, u32[]{:S(2)}) copy-start(bf16[1,256,4096]{2,1,0:T(8,128)(2,1)} %param.5) | copy-start | bytes 6291460
  106.3 5.5 %collective-permute-start.2 = (bf16[16,3,32,4,128]{4,3,2,1,0:T(4,128)(2,1)}, bf16[16,3,32,4,128]{4,3,2,1,0:T(4,128)(2,1)S(1)}, u32[]{:S(2)}, u32[]{:S(2)}) collective-permute-start(bf16[16,3,32,4,128]{4,3,2,1,0:T(4,128)(2,1)} %all-to-all-done.2.half), channel_id=1, source_target_pairs={{0,32},{32,0},{1,33},{33,1},{2,34},{34,2},{3,35},{35,3},{4,36},{36... | collective-permute-start | bytes 4718600 | tf_op jit(solution)/shard_map/ppermute | solution.py:173

commit v2 on v1

--- a/solution.py
+++ b/solution.py
@@ -1,4 +1,3 @@
-import functools
 import math
 
 import jax
@@ -11,6 +10,9 @@
 
 PLANE = ("y", "x", "core")
 EDGE = 32
+NEAR = [d for k in range(8) for _ in range(2) for d in ((k, -k) if k else (0, 8))]
+FAR = [d for k in range(8) for _ in range(2) for d in ((16 - k, k - 16) if k else (16, -8))]
+SHIFTS = (NEAR, FAR)
 CHUNK = 512
 SMALL = pltpu.CompilerParams(vmem_limit_bytes=16 * 1024 * 1024)
 
@@ -57,42 +59,34 @@
     )(scalars, slots, left, right)
 
 
-def weave_kernel(core, half, other, weight):
-    chips, heads, parts = half.shape[:3]
-
-    def one(part, carry):
-        for at in range(chips):
-            for head in range(heads):
-                weight[head, part, 2 * at + core[0]] = half[at, head, part]
-                weight[head, part, 2 * at + 1 - core[0]] = other[at, head, part]
-        return carry
-
-    lax.fori_loop(0, parts, one, 0)
-
-
-def weave(core, half, other):
-    chips, heads, parts, deep, lanes = half.shape
-    return pl.pallas_call(
-        weave_kernel,
-        out_shape=jax.ShapeDtypeStruct((heads, parts, 2 * chips, deep, lanes), jnp.bfloat16),
-        in_specs=[pl.BlockSpec(memory_space=pltpu.SMEM)]
-        + [pl.BlockSpec(memory_space=pltpu.VMEM)] * 2,
-        out_specs=pl.BlockSpec(memory_space=pltpu.VMEM),
-        compiler_params=SMALL,
-        name="weave",
-    )(core, half, other)
-
-
-def attend_kernel(scalars, owned, weight, ends, attended):
+def attend_kernel(scalars, owned, half, other, ends, attended, weight):
     rows = owned.shape[0]
     head_dim = attended.shape[1]
-    start, count = scalars[0], scalars[1]
-    pair = jnp.concatenate([weight[0], weight[1]], axis=1)
-    both = jnp.dot(owned[...], pair, preferred_element_type=jnp.float32).astype(jnp.bfloat16)
-    values = jnp.dot(owned[...], weight[2], preferred_element_type=jnp.float32).astype(
+    shift, count, core, plane, index = (scalars[i] for i in range(5))
+    chips, tiles = half.shape[0], half.shape[1] // 2
+    planes, deep = chips * 2, tiles // 3
+    before = jnp.zeros(half.shape[2:], jnp.float32)
+    for chip in range(chips):
+        for side, block in ((core, half), (1 - core, other)):
+            for kind in range(2):
+                north, south = (SHIFTS[kind][2 * chip + c] for c in range(2))
+                shard = lax.rem(plane + planes - jnp.where(side == 0, north, south), planes)
+                for at in range(deep):
+                    for part in range(3):
+                        weight[part, 2 * shard + chip % 2, at] = block[
+                            chip, kind * tiles + at * 3 + part
+                        ]
+            before += jnp.where(
+                2 * chip + side < index, block[chip, 2 * tiles].astype(jnp.float32), 0.0
+            )
+    start = before[:1, :1].astype(jnp.int32) + shift
+    flat = jnp.concatenate(
+        [weight[part].reshape(-1, head_dim) for part in range(3)], axis=1
+    )
+    projected = jnp.dot(owned[...], flat, preferred_element_type=jnp.float32).astype(
         jnp.bfloat16
     )
-    query, keys = both[:, :head_dim], both[:, head_dim:]
+    query, keys, values = (projected[:, i * head_dim : (i + 1) * head_dim] for i in range(3))
     scores = lax.dot_general(
         query, keys, (((1,), (1,)), ((), ())), preferred_element_type=jnp.float32
     ) / math.sqrt(head_dim)
@@ -111,31 +105,32 @@
     attended[...] = jnp.where(live, result, 0.0).astype(jnp.bfloat16)
 
 
-def attend(scalars, owned, weight, ends):
-    rows, head_dim = owned.shape[0], weight.shape[2]
+def attend(scalars, owned, half, other, ends):
+    chips, tiles, deep, lanes = half.shape
     return pl.pallas_call(
         attend_kernel,
-        out_shape=jax.ShapeDtypeStruct((rows, head_dim), jnp.bfloat16),
+        out_shape=jax.ShapeDtypeStruct((owned.shape[0], lanes), jnp.bfloat16),
         in_specs=[pl.BlockSpec(memory_space=pltpu.SMEM)]
-        + [pl.BlockSpec(memory_space=pltpu.VMEM)] * 3,
+        + [pl.BlockSpec(memory_space=pltpu.VMEM)] * 4,
         out_specs=pl.BlockSpec(memory_space=pltpu.VMEM),
+        scratch_shapes=[pltpu.VMEM((3, 4 * chips, tiles // 6, deep, lanes), jnp.bfloat16)],
         compiler_params=SMALL,
         name="attend",
-    )(scalars, owned, weight, ends)
+    )(scalars, owned, half, other, ends)
 
 
 def for_each(value, count):
     return jnp.broadcast_to(value[None], (count, *value.shape))
 
 
-def weight_column(own):
-    index = lax.axis_index(PLANE)
-    deep = own.shape[0] // lax.axis_size(PLANE)
-    lanes = own.shape[1] // 3
-    piece = lax.dynamic_slice_in_dim(own, index * deep, deep, 0)
-    piece = piece.reshape(deep, 3, lanes).transpose(1, 0, 2)
-    column = lax.all_to_all(for_each(piece, lax.axis_size("z")), "z", 0, 0, tiled=True)
-    return column.transpose(1, 0, 2, 3)
+def moved(value, kind):
+    planes = lax.axis_size("z")
+    pairs = [
+        (j * planes + z, j * planes + (z + shift) % planes)
+        for j, shift in enumerate(SHIFTS[kind])
+        for z in range(planes)
+    ]
+    return lax.ppermute(value, (*PLANE, "z"), pairs)
 
 
 def shards(hidden, pad_counts, doc_lengths, range_shift, qkv_weight):
@@ -145,21 +140,22 @@
     padding = pad_counts[0, 0]
     live = rows - padding
 
-    column = weight_column(qkv_weight)
-
+    deep = qkv_weight.shape[0] // 2
+    own = lax.dynamic_slice_in_dim(qkv_weight, lax.axis_index("x") % 2 * deep, deep, 0)
+    own = own.reshape(deep // 8, 8, 3, -1).transpose(0, 2, 1, 3)
+    own = own.reshape(deep // 8 * 3, 8, -1)
+    far = moved(own, 1)
     head = lax.dynamic_slice_in_dim(slots, padding, EDGE, 0)
     tail = slots[rows - EDGE :]
     left = lax.ppermute(tail, PLANE, [(i, i + 1) for i in range(size - 1)])
     right = lax.ppermute(head, PLANE, [(i + 1, i) for i in range(size - 1)])
-    counts = lax.all_to_all(
-        jnp.broadcast_to(live, (size, 1)), PLANE, 0, 0, tiled=True
-    )[:, 0]
-    column, counts = lax.optimization_barrier((column, counts))
+    near = moved(own, 0)
 
     chips = lax.axis_size(("y", "x"))
-    half = lax.all_to_all(for_each(column, chips), ("y", "x"), 0, 0, tiled=True)
-
-    token_start = jnp.sum(jnp.where(jnp.arange(size) < index, counts, 0))
+    tally = jnp.full((1, *own.shape[1:]), live).astype(jnp.bfloat16)
+    half = lax.all_to_all(
+        for_each(jnp.concatenate([near, far, tally]), chips), ("y", "x"), 0, 0, tiled=True
+    )
     shifts = range_shift[0]
     shift = jnp.where(index == 0, 0, shifts[index])
     following = jnp.where(index == size - 1, 0, shifts[jnp.minimum(index + 1, size - 1)])
@@ -167,14 +163,13 @@
     scalars = jnp.stack([padding, live, shift, count]).astype(jnp.int32)
     owned = gather_rows(scalars, slots, left, right)
     ends = jnp.cumsum(doc_lengths[0])[None]
-    where = jnp.stack([token_start + shift, count]).astype(jnp.int32)
+    where = jnp.stack(
+        [shift, count, lax.axis_index("core"), lax.axis_index("z"), index]
+    ).astype(jnp.int32)
     half, owned, ends, where = lax.optimization_barrier((half, owned, ends, where))
 
     other = lax.ppermute(half, "core", [(0, 1), (1, 0)])
-    core = lax.axis_index("core").reshape(1)
-    weight = weave(core, half, other)
-    weight = weight.reshape(3, -1, weight.shape[-1])
-    return attend(where, owned, weight, ends)[None]
+    return attend(where, owned, half, other, ends)[None]
 
 
 def solution(mesh):

time: 118 us -> 87.8 us (0.74)
  the two profiles are of different devices: /device:TPU:1 before, /device:TPU:23 now
where the time goes in v2:
time: 87.8 us; the launch traced here: 87.4 us
  starting transfers between devices  53.2 us (61%)
  waiting for transfers between devices  19.8 us (23%)
  Pallas kernels  6.19 us (7%)
  local copies, waits for them, and re-layouts  5.79 us (7%)
  between operations  1.98 us (2%)
    ppermute x2, starting transfers between devices, moved(): return lax.ppermute(value, (*PLANE, 'z'), pairs)  30.9 us
    ppermute x1, waiting for transfers between devices, shards(): right = lax.ppermute(head, PLANE, [(i + 1, i) for i in range(size - 1)])  13 us
    all_to_all x1, starting transfers between devices, shards(): lax.all_to_all(for_each(jnp.concatenate([near, far, tally]), chips), ('y'...  7.72 us
    ppermute x1, starting transfers between devices, shards(): other = lax.ppermute(half, 'core', [(0, 1), (1, 0)])  6.94 us
    ppermute x1, starting transfers between devices, shards(): left = lax.ppermute(tail, PLANE, [(i, i + 1) for i in range(size - 1)])  5.73 us
    pallas_call x1, Pallas kernels, attend(): pl.pallas_call(attend_kernel, out_shape=jax.ShapeDtypeStruct((owned.shape...  4.41 us
    ppermute x2, waiting for transfers between devices, moved(): return lax.ppermute(value, (*PLANE, 'z'), pairs)  3.51 us
    ppermute x1, waiting for transfers between devices, shards(): other = lax.ppermute(half, 'core', [(0, 1), (1, 0)])  3.27 us
  transfers between devices with their start and end apart: 6, of which 3 were waited for; matrix products, arithmetic and copies ran while one was open for 3% of the time, Pallas kernels for 2%

profile of v2, /device:TPU:23, one launch (start us, length us, event | category | flops | bytes accessed | tf_op | source)
XLA Modules:
  0.0 87.4 jit_solution(17770397458043751073)
XLA Ops:
  0.0 0.0 copy-start
  0.0 0.9 %copy-done = bf16[128,384]{1,0:T(8,128)(2,1)S(1)} copy-done((bf16[128,384]{1,0:T(8,128)(2,1)S(1)}, bf16[128,384]{1,0:T(8,128)(2,1)}, u32[]{:S(2)}) %copy-start) | copy-done | bytes 98328
  0.9 25.2 %collective-permute-start.1 = (bf16[24,8,128]{2,1,0:T(8,128)(2,1)S(1)}, bf16[24,8,128]{2,1,0:T(8,128)(2,1)S(1)}, u32[]{:S(2)}, u32[]{:S(2)}) collective-permute-start(bf16[24,8,128]{2,1,0:T(8,128)(2,1)S(1)} %bitcast.28), channel_id=1, source_target_pairs={{0,16},{1,17},{2,18},{3,19},{4,20},{5,21},{6,22},{7,23},{8,24},{9,... | collective-permute-start | bytes 147464 | tf_op jit(solution)/shard_map/ppermute | solution.py:133
  26.2 5.6 %collective-permute-start = (bf16[24,8,128]{2,1,0:T(8,128)(2,1)S(1)}, bf16[24,8,128]{2,1,0:T(8,128)(2,1)S(1)}, u32[]{:S(2)}, u32[]{:S(2)}) collective-permute-start(bf16[24,8,128]{2,1,0:T(8,128)(2,1)S(1)} %bitcast.29), channel_id=1, source_target_pairs={{0,0},{1,1},{2,2},{3,3},{4,4},{5,5},{6,6},{7,7},{8,8},{9,9},{10,10... | collective-permute-start | bytes 147464 | tf_op jit(solution)/shard_map/ppermute | solution.py:133
  32.4 0.1 pad.6.clone
  32.5 0.0 collective-permute-done.1
  32.5 3.5 %collective-permute-done = bf16[24,8,128]{2,1,0:T(8,128)(2,1)S(1)} collective-permute-done((bf16[24,8,128]{2,1,0:T(8,128)(2,1)S(1)}, bf16[24,8,128]{2,1,0:T(8,128)(2,1)S(1)}, u32[]{:S(2)}, u32[]{:S(2)}) %collective-permute-start) | collective-permute-done | bytes 49184 | tf_op jit(solution)/shard_map/ppermute | solution.py:133
  36.0 0.1 maximum_maximum_fusion
  36.2 1.4 %broadcast_in_dim.14 = bf16[16,49,8,128]{3,2,1,0:T(8,128)(2,1)} broadcast(bf16[49,8,128]{2,1,0:T(8,128)(2,1)S(1)} %maximum_maximum_fusion), dimensions={1,2,3} | broadcast | bytes 1705984 | tf_op jit(solution)/shard_map/broadcast_in_dim | solution.py:123
  37.5 0.0 copy-start.2
  37.5 0.0 copy-start.3
  37.5 7.7 %all-to-all-start = ((bf16[16,49,8,128]{3,2,1,0:T(8,128)(2,1)}), bf16[16,49,8,128]{3,2,1,0:T(8,128)(2,1)}, u32[]{:S(2)}, u32[]{:S(2)}) async-start(bf16[16,49,8,128]{3,2,1,0:T(8,128)(2,1)} %broadcast_in_dim.14), calls=%async_computation | async-start | bytes 3211264 | tf_op jit(solution)/shard_map/all_to_all | solution.py:156
  45.2 1.1 %dynamic-slice_bitcast_fusion = (bf16[32,4096]{1,0:T(8,128)(2,1)S(1)}, bf16[32,4096]{1,0:T(8,128)(2,1)S(1)}) fusion(bf16[1,256,4096]{2,1,0:T(8,128)(2,1)} %param.5, s32[]{:T(128)S(6)} %select_n.32), kind=kLoop, calls=%fused_computation | loop fusion | bytes 1048580 | tf_op jit(solution)/shard_map/dynamic_slice | solution.py:148
  46.4 1.9 %collective-permute-start.3 = (bf16[32,4096]{1,0:T(8,128)(2,1)S(1)}, bf16[32,4096]{1,0:T(8,128)(2,1)S(1)}, u32[]{:S(2)}, u32[]{:S(2)}) collective-permute-start(bf16[32,4096]{1,0:T(8,128)(2,1)S(1)} %get-tuple-element.13), channel_id=1, source_target_pairs={{32,0},{64,32},{96,64},{128,96},{160,128},{192,160},{224,192},{256... | collective-permute-start | bytes 786440 | tf_op jit(solution)/shard_map/ppermute | solution.py:151
  48.3 5.7 %collective-permute-start.2 = (bf16[32,4096]{1,0:T(8,128)(2,1)S(1)}, bf16[32,4096]{1,0:T(8,128)(2,1)S(1)}, u32[]{:S(2)}, u32[]{:S(2)}) collective-permute-start(bf16[32,4096]{1,0:T(8,128)(2,1)S(1)} %get-tuple-element.14), channel_id=1, source_target_pairs={{0,32},{32,64},{64,96},{96,128},{128,160},{160,192},{192,224},{224... | collective-permute-start | bytes 786440 | tf_op jit(solution)/shard_map/ppermute | solution.py:150
  54.1 0.0 copy-done.2
  54.1 0.7 constant_dynamic-slice_fusion.1
  55.4 0.0 copy-done.3
  55.4 0.3 reduce-window_clone.1.ends
  56.3 0.1 stack.33.scalars
  56.3 0.1 pad_add_fusion.scalars
  56.4 13.0 %collective-permute-done.3.right = bf16[32,4096]{1,0:T(8,128)(2,1)S(1)} collective-permute-done((bf16[32,4096]{1,0:T(8,128)(2,1)S(1)}, bf16[32,4096]{1,0:T(8,128)(2,1)S(1)}, u32[]{:S(2)}, u32[]{:S(2)}) %collective-permute-start.3) | collective-permute-done | bytes 262176 | tf_op jit(solution)/shard_map/ppermute | solution.py:151
  69.4 0.0 collective-permute-done.2.left
  69.4 0.0 copy-start.1
  69.4 1.6 %copy-done.1 = bf16[1,256,4096]{2,1,0:T(8,128)(2,1)S(1)} copy-done((bf16[1,256,4096]{2,1,0:T(8,128)(2,1)S(1)}, bf16[1,256,4096]{2,1,0:T(8,128)(2,1)}, u32[]{:S(2)}) %copy-start.1) | copy-done | bytes 2097176
  71.0 1.8 %gather_rows.1.owned = bf16[256,4096]{1,0:T(8,128)(2,1)S(1)} custom-call(s32[4]{0:T(128)S(1)} %pad_add_fusion.scalars, bf16[256,4096]{1,0:T(8,128)(2,1)S(1)} %bitcast.27, bf16[32,4096]{1,0:T(8,128)(2,1)S(1)} %collective-permute-done.2.left, bf16[32,4096]{1,0:T(8,128)(2,1)S(1)} %collective-permute-done.3.right), custom_call_target="tpu_custom_call" | custom-call | flops 671088640 | bytes 4194304 | tf_op jit(solution)/shard_map/gather_rows/pallas_call | solution.py:46
  72.8 0.0 all-to-all-done.half
  72.8 6.9 %collective-permute-start.4 = (bf16[16,49,8,128]{3,2,1,0:T(8,128)(2,1)}, bf16[16,49,8,128]{3,2,1,0:T(8,128)(2,1)S(1)}, u32[]{:S(2)}, u32[]{:S(2)}) collective-permute-start(bf16[16,49,8,128]{3,2,1,0:T(8,128)(2,1)} %all-to-all-done.half), channel_id=1, source_target_pairs={{0,32},{32,0},{1,33},{33,1},{2,34},{34,2},{3,35},{35,3},{4,36},{36... | collective-permute-start | bytes 4816904 | tf_op jit(solution)/shard_map/ppermute | solution.py:171
  79.7 3.3 %collective-permute-done.4.other = bf16[16,49,8,128]{3,2,1,0:T(8,128)(2,1)S(1)} collective-permute-done((bf16[16,49,8,128]{3,2,1,0:T(8,128)(2,1)}, bf16[16,49,8,128]{3,2,1,0:T(8,128)(2,1)S(1)}, u32[]{:S(2)}, u32[]{:S(2)}) %collective-permute-start.4) | collective-permute-done | bytes 1605664 | tf_op jit(solution)/shard_map/ppermute | solution.py:171
  83.0 4.4 %attend.1 = bf16[256,128]{1,0:T(8,128)(2,1)} custom-call(s32[5]{0:T(128)S(1)} %stack.33.scalars, bf16[256,4096]{1,0:T(8,128)(2,1)S(1)} %gather_rows.1.owned, bf16[16,49,8,128]{3,2,1,0:T(8,128)(2,1)} %all-to-all-done.half, bf16[16,49,8,128]{3,2,1,0:T(8,128)(2,1)S(1)} %collective-permute-done.4.other, s32[1,128]{1,0:T(1,128)S(1)} %reduce-window_clone.1.ends), custom_call_target="tpu_custom_call" | custom-call | tf_op jit(solution)/shard_map/attend/pallas_call | solution.py:110
  (1 shorter events, 0.0 us)
Async XLA Ops:
  0.0 0.9 %copy-start = (bf16[128,384]{1,0:T(8,128)(2,1)S(1)}, bf16[128,384]{1,0:T(8,128)(2,1)}, u32[]{:S(2)}) copy-start(bf16[128,384]{1,0:T(8,128)(2,1)} %param.9) | copy-start | bytes 294916
  0.9 31.6 %collective-permute-start.1 = (bf16[24,8,128]{2,1,0:T(8,128)(2,1)S(1)}, bf16[24,8,128]{2,1,0:T(8,128)(2,1)S(1)}, u32[]{:S(2)}, u32[]{:S(2)}) collective-permute-start(bf16[24,8,128]{2,1,0:T(8,128)(2,1)S(1)} %bitcast.28), channel_id=1, source_target_pairs={{0,16},{1,17},{2,18},{3,19},{4,20},{5,21},{6,22},{7,23},{8,24},{9,... | collective-permute-start | bytes 147464 | tf_op jit(solution)/shard_map/ppermute | solution.py:133
  26.2 9.9 %collective-permute-start = (bf16[24,8,128]{2,1,0:T(8,128)(2,1)S(1)}, bf16[24,8,128]{2,1,0:T(8,128)(2,1)S(1)}, u32[]{:S(2)}, u32[]{:S(2)}) collective-permute-start(bf16[24,8,128]{2,1,0:T(8,128)(2,1)S(1)} %bitcast.29), channel_id=1, source_target_pairs={{0,0},{1,1},{2,2},{3,3},{4,4},{5,5},{6,6},{7,7},{8,8},{9,9},{10,10... | collective-permute-start | bytes 147464 | tf_op jit(solution)/shard_map/ppermute | solution.py:133
  37.5 16.5 %copy-start.2 = (s32[1,32]{1,0:T(1,128)S(1)}, s32[1,32]{1,0:T(1,128)}, u32[]{:S(2)}) copy-start(s32[1,32]{1,0:T(1,128)} %param.8) | copy-start | bytes 388
  37.5 17.9 %copy-start.3 = (s32[1,128]{1,0:T(1,128)S(1)}, s32[1,128]{1,0:T(1,128)}, u32[]{:S(2)}) copy-start(s32[1,128]{1,0:T(1,128)} %param.7) | copy-start | bytes 1540
  37.5 35.3 %all-to-all-start = ((bf16[16,49,8,128]{3,2,1,0:T(8,128)(2,1)}), bf16[16,49,8,128]{3,2,1,0:T(8,128)(2,1)}, u32[]{:S(2)}, u32[]{:S(2)}) async-start(bf16[16,49,8,128]{3,2,1,0:T(8,128)(2,1)} %broadcast_in_dim.14), calls=%async_computation | async-start | bytes 3211264 | tf_op jit(solution)/shard_map/all_to_all | solution.py:156
  46.4 23.0 %collective-permute-start.3 = (bf16[32,4096]{1,0:T(8,128)(2,1)S(1)}, bf16[32,4096]{1,0:T(8,128)(2,1)S(1)}, u32[]{:S(2)}, u32[]{:S(2)}) collective-permute-start(bf16[32,4096]{1,0:T(8,128)(2,1)S(1)} %get-tuple-element.13), channel_id=1, source_target_pairs={{32,0},{64,32},{96,64},{128,96},{160,128},{192,160},{224,192},{256... | collective-permute-start | bytes 786440 | tf_op jit(solution)/shard_map/ppermute | solution.py:151
  48.3 21.1 %collective-permute-start.2 = (bf16[32,4096]{1,0:T(8,128)(2,1)S(1)}, bf16[32,4096]{1,0:T(8,128)(2,1)S(1)}, u32[]{:S(2)}, u32[]{:S(2)}) collective-permute-start(bf16[32,4096]{1,0:T(8,128)(2,1)S(1)} %get-tuple-element.14), channel_id=1, source_target_pairs={{0,32},{32,64},{64,96},{96,128},{128,160},{160,192},{192,224},{224... | collective-permute-start | bytes 786440 | tf_op jit(solution)/shard_map/ppermute | solution.py:150
  69.4 1.6 %copy-start.1 = (bf16[1,256,4096]{2,1,0:T(8,128)(2,1)S(1)}, bf16[1,256,4096]{2,1,0:T(8,128)(2,1)}, u32[]{:S(2)}) copy-start(bf16[1,256,4096]{2,1,0:T(8,128)(2,1)} %param.5) | copy-start | bytes 6291460
  72.8 10.2 %collective-permute-start.4 = (bf16[16,49,8,128]{3,2,1,0:T(8,128)(2,1)}, bf16[16,49,8,128]{3,2,1,0:T(8,128)(2,1)S(1)}, u32[]{:S(2)}, u32[]{:S(2)}) collective-permute-start(bf16[16,49,8,128]{3,2,1,0:T(8,128)(2,1)} %all-to-all-done.half), channel_id=1, source_target_pairs={{0,32},{32,0},{1,33},{33,1},{2,34},{34,2},{3,35},{35,3},{4,36},{36... | collective-permute-start | bytes 4816904 | tf_op jit(solution)/shard_map/ppermute | solution.py:171

commit v3 on v2

--- a/solution.py
+++ b/solution.py
@@ -14,6 +14,7 @@
 FAR = [d for k in range(8) for _ in range(2) for d in ((16 - k, k - 16) if k else (16, -8))]
 SHIFTS = (NEAR, FAR)
 CHUNK = 512
+LANES = 128
 SMALL = pltpu.CompilerParams(vmem_limit_bytes=16 * 1024 * 1024)
 
 
@@ -35,17 +36,19 @@
     for at in range(0, slots.shape[1], CHUNK):
         columns = slice(at, at + CHUNK)
         edges = jnp.concatenate([left[:, columns], right[:, columns]], axis=0)
-        owned[:, columns] = (
+        picked = (
             jnp.dot(pick_here, slots[:, columns], preferred_element_type=jnp.float32)
             + jnp.dot(pick_edge, edges, preferred_element_type=jnp.float32)
         ).astype(jnp.bfloat16)
+        for lane in range(0, CHUNK, LANES):
+            owned[(at + lane) // LANES] = picked[:, lane : lane + LANES]
 
 
 def gather_rows(scalars, slots, left, right):
     rows, width = slots.shape
     return pl.pallas_call(
         gather_kernel,
-        out_shape=jax.ShapeDtypeStruct((rows, width), jnp.bfloat16),
+        out_shape=jax.ShapeDtypeStruct((width // LANES, rows, LANES), jnp.bfloat16),
         in_specs=[pl.BlockSpec(memory_space=pltpu.SMEM)]
         + [pl.BlockSpec(memory_space=pltpu.VMEM)] * 3,
         out_specs=pl.BlockSpec(memory_space=pltpu.VMEM),
@@ -59,31 +62,74 @@
     )(scalars, slots, left, right)
 
 
-def attend_kernel(scalars, owned, half, other, ends, attended, weight):
-    rows = owned.shape[0]
+def project_half(side, plane, owned, block):
+    planes, _, _ = owned.shape
+    deep = (block.shape[1] - 8) // 6
+    total = None
+    for pair in range(block.shape[0] // 2):
+        inputs, weights = [], []
+        for kind in range(2):
+            north, south = (SHIFTS[kind][4 * pair + c] for c in range(2))
+            shard = lax.rem(plane + planes - jnp.where(side == 0, north, south), planes)
+            inputs.append(owned[shard])
+            at = kind * 3 * deep
+            for chip in (2 * pair, 2 * pair + 1):
+                weights.append(
+                    jnp.concatenate(
+                        [block[chip, at + i * deep : at + (i + 1) * deep] for i in range(3)],
+                        axis=1,
+                    )
+                )
+        part = jnp.dot(
+            jnp.concatenate(inputs, axis=1),
+            jnp.concatenate(weights, axis=0),
+            preferred_element_type=jnp.float32,
+        )
+        total = part if total is None else total + part
+    return total
+
+
+def tokens_before(side, index, block):
+    last = block.shape[1] - 8
+    total = jnp.zeros((8, block.shape[2]), jnp.float32)
+    for chip in range(block.shape[0]):
+        total += jnp.where(2 * chip + side < index, block[chip, last:].astype(jnp.float32), 0.0)
+    return total
+
+
+def project_kernel(scalars, owned, half, projected, before):
+    core, plane, index = (scalars[i] for i in range(2, 5))
+    projected[...] = project_half(core, plane, owned, half)
+    before[...] = tokens_before(core, index, half)
+
+
+def project(scalars, owned, half):
+    _, rows, lanes = owned.shape
+    chips, deep, width = half.shape[0], (half.shape[1] - 8) // 6, 3 * lanes
+    return pl.pallas_call(
+        project_kernel,
+        out_shape=(
+            jax.ShapeDtypeStruct((rows, width), jnp.float32),
+            jax.ShapeDtypeStruct((8, lanes), jnp.float32),
+        ),
+        in_specs=[pl.BlockSpec(memory_space=pltpu.SMEM)]
+        + [pl.BlockSpec(memory_space=pltpu.VMEM)] * 2,
+        out_specs=(pl.BlockSpec(memory_space=pltpu.VMEM),) * 2,
+        compiler_params=SMALL,
+        cost_estimate=pl.CostEstimate(
+            flops=4 * rows * chips * deep * width, bytes_accessed=0, transcendentals=0
+        ),
+        name="project",
+    )(scalars, owned, half)
+
+
+def attend_kernel(scalars, owned, projected, before, other, ends, attended):
+    rows = owned.shape[1]
     head_dim = attended.shape[1]
     shift, count, core, plane, index = (scalars[i] for i in range(5))
-    chips, tiles = half.shape[0], half.shape[1] // 2
-    planes, deep = chips * 2, tiles // 3
-    before = jnp.zeros(half.shape[2:], jnp.float32)
-    for chip in range(chips):
-        for side, block in ((core, half), (1 - core, other)):
-            for kind in range(2):
-                north, south = (SHIFTS[kind][2 * chip + c] for c in range(2))
-                shard = lax.rem(plane + planes - jnp.where(side == 0, north, south), planes)
-                for at in range(deep):
-                    for part in range(3):
-                        weight[part, 2 * shard + chip % 2, at] = block[
-                            chip, kind * tiles + at * 3 + part
-                        ]
-            before += jnp.where(
-                2 * chip + side < index, block[chip, 2 * tiles].astype(jnp.float32), 0.0
-            )
+    before = before[...] + tokens_before(1 - core, index, other)
     start = before[:1, :1].astype(jnp.int32) + shift
-    flat = jnp.concatenate(
-        [weight[part].reshape(-1, head_dim) for part in range(3)], axis=1
-    )
-    projected = jnp.dot(owned[...], flat, preferred_element_type=jnp.float32).astype(
+    projected = (projected[...] + project_half(1 - core, plane, owned, other)).astype(
         jnp.bfloat16
     )
     query, keys, values = (projected[:, i * head_dim : (i + 1) * head_dim] for i in range(3))
@@ -105,18 +151,16 @@
     attended[...] = jnp.where(live, result, 0.0).astype(jnp.bfloat16)
 
 
-def attend(scalars, owned, half, other, ends):
-    chips, tiles, deep, lanes = half.shape
+def attend(scalars, owned, projected, before, other, ends):
     return pl.pallas_call(
         attend_kernel,
-        out_shape=jax.ShapeDtypeStruct((owned.shape[0], lanes), jnp.bfloat16),
+        out_shape=jax.ShapeDtypeStruct(owned.shape[1:], jnp.bfloat16),
         in_specs=[pl.BlockSpec(memory_space=pltpu.SMEM)]
-        + [pl.BlockSpec(memory_space=pltpu.VMEM)] * 4,
+        + [pl.BlockSpec(memory_space=pltpu.VMEM)] * 5,
         out_specs=pl.BlockSpec(memory_space=pltpu.VMEM),
-        scratch_shapes=[pltpu.VMEM((3, 4 * chips, tiles // 6, deep, lanes), jnp.bfloat16)],
         compiler_params=SMALL,
         name="attend",
-    )(scalars, owned, half, other, ends)
+    )(scalars, owned, projected, before, other, ends)
 
 
 def for_each(value, count):
@@ -142,8 +186,7 @@
 
     deep = qkv_weight.shape[0] // 2
     own = lax.dynamic_slice_in_dim(qkv_weight, lax.axis_index("x") % 2 * deep, deep, 0)
-    own = own.reshape(deep // 8, 8, 3, -1).transpose(0, 2, 1, 3)
-    own = own.reshape(deep // 8 * 3, 8, -1)
+    own = jnp.concatenate(jnp.split(own, 3, axis=1), axis=0)
     far = moved(own, 1)
     head = lax.dynamic_slice_in_dim(slots, padding, EDGE, 0)
     tail = slots[rows - EDGE :]
@@ -152,7 +195,7 @@
     near = moved(own, 0)
 
     chips = lax.axis_size(("y", "x"))
-    tally = jnp.full((1, *own.shape[1:]), live).astype(jnp.bfloat16)
+    tally = jnp.full((8, own.shape[1]), live).astype(jnp.bfloat16)
     half = lax.all_to_all(
         for_each(jnp.concatenate([near, far, tally]), chips), ("y", "x"), 0, 0, tiled=True
     )
@@ -169,7 +212,8 @@
     half, owned, ends, where = lax.optimization_barrier((half, owned, ends, where))
 
     other = lax.ppermute(half, "core", [(0, 1), (1, 0)])
-    return attend(where, owned, half, other, ends)[None]
+    projected, before = project(where, owned, half)
+    return attend(where, owned, projected, before, other, ends)[None]
 
 
 def solution(mesh):

time: 87.8 us -> 84 us (0.957)
  the two profiles are of different devices: /device:TPU:23 before, /device:TPU:87 now
where the time goes in v3:
time: 84 us; the launch traced here: 83.5 us
  starting transfers between devices  45.3 us (54%)
  waiting for transfers between devices  23.9 us (28%)
  Pallas kernels  6.3 us (8%)
  local copies, waits for them, and re-layouts  5.58 us (7%)
  between operations  2.01 us (2%)
    ppermute x2, starting transfers between devices, moved(): return lax.ppermute(value, (*PLANE, 'z'), pairs)  29.1 us
    ppermute x1, waiting for transfers between devices, shards(): left = lax.ppermute(tail, PLANE, [(i, i + 1) for i in range(size - 1)])  11 us
    ppermute x2, waiting for transfers between devices, moved(): return lax.ppermute(value, (*PLANE, 'z'), pairs)  8.2 us
    all_to_all x1, starting transfers between devices, shards(): lax.all_to_all(for_each(jnp.concatenate([near, far, tally]), chips), ('y'...  6.77 us
    ppermute x1, starting transfers between devices, shards(): other = lax.ppermute(half, 'core', [(0, 1), (1, 0)])  5.1 us
    ppermute x1, waiting for transfers between devices, shards(): right = lax.ppermute(head, PLANE, [(i + 1, i) for i in range(size - 1)])  3.5 us
    ppermute x1, starting transfers between devices, shards(): right = lax.ppermute(head, PLANE, [(i + 1, i) for i in range(size - 1)])  2.41 us
    pallas_call x1, Pallas kernels, attend(): pl.pallas_call(attend_kernel, out_shape=jax.ShapeDtypeStruct(owned.shape[...  2.38 us
  transfers between devices with their start and end apart: 6, of which 4 were waited for; matrix products, arithmetic and copies ran while one was open for 3% of the time, Pallas kernels for 5%

profile of v3, /device:TPU:87, one launch (start us, length us, event | category | flops | bytes accessed | tf_op | source)
XLA Modules:
  0.0 83.5 jit_solution(1681688671600063315)
XLA Ops:
  0.0 0.8 constant_dynamic-slice_fusion
  0.8 18.4 %collective-permute-start = (bf16[192,128]{1,0:T(8,128)(2,1)S(1)}, bf16[192,128]{1,0:T(8,128)(2,1)S(1)}, u32[]{:S(2)}, u32[]{:S(2)}) collective-permute-start(bf16[192,128]{1,0:T(8,128)(2,1)S(1)} %pad_maximum_fusion), channel_id=1, source_target_pairs={{0,0},{1,1},{2,2},{3,3},{4,4},{5,5},{6,6},{7,7},{8,8},{9,9},{10,10... | collective-permute-start | bytes 147464 | tf_op jit(solution)/shard_map/ppermute | solution.py:177
  19.1 10.7 %collective-permute-start.1 = (bf16[192,128]{1,0:T(8,128)(2,1)S(1)}, bf16[192,128]{1,0:T(8,128)(2,1)S(1)}, u32[]{:S(2)}, u32[]{:S(2)}) collective-permute-start(bf16[192,128]{1,0:T(8,128)(2,1)S(1)} %pad_maximum_fusion), channel_id=1, source_target_pairs={{0,16},{1,17},{2,18},{3,19},{4,20},{5,21},{6,22},{7,23},{8,24},{9,... | collective-permute-start | bytes 147464 | tf_op jit(solution)/shard_map/ppermute | solution.py:177
  30.5 0.0 collective-permute-done
  30.6 8.2 %collective-permute-done.1 = bf16[192,128]{1,0:T(8,128)(2,1)S(1)} collective-permute-done((bf16[192,128]{1,0:T(8,128)(2,1)S(1)}, bf16[192,128]{1,0:T(8,128)(2,1)S(1)}, u32[]{:S(2)}, u32[]{:S(2)}) %collective-permute-start.1) | collective-permute-done | bytes 49184 | tf_op jit(solution)/shard_map/ppermute | solution.py:177
  38.8 0.1 maximum_maximum_fusion
  38.9 1.4 %broadcast_in_dim.14 = bf16[16,392,128]{2,1,0:T(8,128)(2,1)} broadcast(bf16[392,128]{1,0:T(8,128)(2,1)S(1)} %maximum_maximum_fusion), dimensions={1,2} | broadcast | bytes 1705984 | tf_op jit(solution)/shard_map/broadcast_in_dim | solution.py:167
  40.2 0.0 copy-start.1
  40.2 0.0 copy-start.2
  40.2 6.8 %all-to-all-start = ((bf16[16,392,128]{2,1,0:T(8,128)(2,1)}), bf16[16,392,128]{2,1,0:T(8,128)(2,1)}, u32[]{:S(2)}, u32[]{:S(2)}) async-start(bf16[16,392,128]{2,1,0:T(8,128)(2,1)} %broadcast_in_dim.14), calls=%async_computation | async-start | bytes 3211264 | tf_op jit(solution)/shard_map/all_to_all | solution.py:199
  47.0 1.1 %dynamic-slice_bitcast_fusion = (bf16[32,4096]{1,0:T(8,128)(2,1)S(1)}, bf16[32,4096]{1,0:T(8,128)(2,1)S(1)}) fusion(bf16[1,256,4096]{2,1,0:T(8,128)(2,1)} %param.5, s32[]{:T(128)S(6)} %select_n.32), kind=kLoop, calls=%fused_computation | loop fusion | bytes 1048580 | tf_op jit(solution)/shard_map/dynamic_slice | solution.py:191
  48.1 1.9 %collective-permute-start.2 = (bf16[32,4096]{1,0:T(8,128)(2,1)S(1)}, bf16[32,4096]{1,0:T(8,128)(2,1)S(1)}, u32[]{:S(2)}, u32[]{:S(2)}) collective-permute-start(bf16[32,4096]{1,0:T(8,128)(2,1)S(1)} %get-tuple-element.18), channel_id=1, source_target_pairs={{0,32},{32,64},{64,96},{96,128},{128,160},{160,192},{192,224},{224... | collective-permute-start | bytes 786440 | tf_op jit(solution)/shard_map/ppermute | solution.py:193
  50.1 2.4 %collective-permute-start.3 = (bf16[32,4096]{1,0:T(8,128)(2,1)S(1)}, bf16[32,4096]{1,0:T(8,128)(2,1)S(1)}, u32[]{:S(2)}, u32[]{:S(2)}) collective-permute-start(bf16[32,4096]{1,0:T(8,128)(2,1)S(1)} %get-tuple-element.17), channel_id=1, source_target_pairs={{32,0},{64,32},{96,64},{128,96},{160,128},{192,160},{224,192},{256... | collective-permute-start | bytes 786440 | tf_op jit(solution)/shard_map/ppermute | solution.py:194
  52.5 0.0 copy-done.1
  52.5 0.7 constant_dynamic-slice_fusion.2
  53.8 0.0 copy-done.2
  53.8 0.3 reduce-window_clone.1.ends
  54.7 0.1 stack.33.scalars
  54.8 0.1 pad_add_fusion.scalars
  54.8 11.0 %collective-permute-done.2.left = bf16[32,4096]{1,0:T(8,128)(2,1)S(1)} collective-permute-done((bf16[32,4096]{1,0:T(8,128)(2,1)S(1)}, bf16[32,4096]{1,0:T(8,128)(2,1)S(1)}, u32[]{:S(2)}, u32[]{:S(2)}) %collective-permute-start.2) | collective-permute-done | bytes 262176 | tf_op jit(solution)/shard_map/ppermute | solution.py:193
  65.9 3.5 %collective-permute-done.3.right = bf16[32,4096]{1,0:T(8,128)(2,1)S(1)} collective-permute-done((bf16[32,4096]{1,0:T(8,128)(2,1)S(1)}, bf16[32,4096]{1,0:T(8,128)(2,1)S(1)}, u32[]{:S(2)}, u32[]{:S(2)}) %collective-permute-start.3) | collective-permute-done | bytes 262176 | tf_op jit(solution)/shard_map/ppermute | solution.py:194
  69.4 0.0 copy-start
  69.4 1.6 %copy-done = bf16[1,256,4096]{2,1,0:T(8,128)(2,1)S(1)} copy-done((bf16[1,256,4096]{2,1,0:T(8,128)(2,1)S(1)}, bf16[1,256,4096]{2,1,0:T(8,128)(2,1)}, u32[]{:S(2)}) %copy-start) | copy-done | bytes 2097176
  71.0 1.8 %gather_rows.1.owned = bf16[32,256,128]{2,1,0:T(8,128)(2,1)S(1)} custom-call(s32[4]{0:T(128)S(1)} %pad_add_fusion.scalars, bf16[256,4096]{1,0:T(8,128)(2,1)S(1)} %bitcast.21, bf16[32,4096]{1,0:T(8,128)(2,1)S(1)} %collective-permute-done.2.left, bf16[32,4096]{1,0:T(8,128)(2,1)S(1)} %collective-permute-done.3.right), custom_call_target="tpu_custom_call" | custom-call | flops 671088640 | bytes 4194304 | tf_op jit(solution)/shard_map/gather_rows/pallas_call | solution.py:49
  72.8 0.0 all-to-all-done.half
  72.8 5.1 %collective-permute-start.4 = (bf16[16,392,128]{2,1,0:T(8,128)(2,1)}, bf16[16,392,128]{2,1,0:T(8,128)(2,1)S(1)}, u32[]{:S(2)}, u32[]{:S(2)}) collective-permute-start(bf16[16,392,128]{2,1,0:T(8,128)(2,1)} %all-to-all-done.half), channel_id=1, source_target_pairs={{0,32},{32,0},{1,33},{33,1},{2,34},{34,2},{3,35},{35,3},{4,36},{36... | collective-permute-start | bytes 4816904 | tf_op jit(solution)/shard_map/ppermute | solution.py:214
  77.9 2.1 %project.1 = (f32[256,384]{1,0:T(8,128)S(1)}, f32[8,128]{1,0:T(8,128)S(1)}) custom-call(s32[5]{0:T(128)S(1)} %stack.33.scalars, bf16[32,256,128]{2,1,0:T(8,128)(2,1)S(1)} %gather_rows.1.owned, bf16[16,392,128]{2,1,0:T(8,128)(2,1)} %all-to-all-done.half), custom_call_target="tpu_custom_call" | custom-call | flops 402653184 | tf_op jit(solution)/shard_map/project/pallas_call | solution.py:109
  80.0 1.1 %collective-permute-done.4.other = bf16[16,392,128]{2,1,0:T(8,128)(2,1)S(1)} collective-permute-done((bf16[16,392,128]{2,1,0:T(8,128)(2,1)}, bf16[16,392,128]{2,1,0:T(8,128)(2,1)S(1)}, u32[]{:S(2)}, u32[]{:S(2)}) %collective-permute-start.4) | collective-permute-done | bytes 1605664 | tf_op jit(solution)/shard_map/ppermute | solution.py:214
  81.2 2.4 %attend.1 = bf16[256,128]{1,0:T(8,128)(2,1)} custom-call(s32[5]{0:T(128)S(1)} %stack.33.scalars, bf16[32,256,128]{2,1,0:T(8,128)(2,1)S(1)} %gather_rows.1.owned, f32[256,384]{1,0:T(8,128)S(1)} %get-tuple-element.14.projected, f32[8,128]{1,0:T(8,128)S(1)} %get-tuple-element.15.before, bf16[16,392,128]{2,1,0:T(8,128)(2,1)S(1)} %collective-permute-done.4.other, ...), custom_call_target="tpu_custom_call" | custom-call | tf_op jit(solution)/shard_map/attend/pallas_call | solution.py:155
  (3 shorter events, 0.0 us)
Async XLA Ops:
  0.8 29.8 %collective-permute-start = (bf16[192,128]{1,0:T(8,128)(2,1)S(1)}, bf16[192,128]{1,0:T(8,128)(2,1)S(1)}, u32[]{:S(2)}, u32[]{:S(2)}) collective-permute-start(bf16[192,128]{1,0:T(8,128)(2,1)S(1)} %pad_maximum_fusion), channel_id=1, source_target_pairs={{0,0},{1,1},{2,2},{3,3},{4,4},{5,5},{6,6},{7,7},{8,8},{9,9},{10,10... | collective-permute-start | bytes 147464 | tf_op jit(solution)/shard_map/ppermute | solution.py:177
  19.1 19.6 %collective-permute-start.1 = (bf16[192,128]{1,0:T(8,128)(2,1)S(1)}, bf16[192,128]{1,0:T(8,128)(2,1)S(1)}, u32[]{:S(2)}, u32[]{:S(2)}) collective-permute-start(bf16[192,128]{1,0:T(8,128)(2,1)S(1)} %pad_maximum_fusion), channel_id=1, source_target_pairs={{0,16},{1,17},{2,18},{3,19},{4,20},{5,21},{6,22},{7,23},{8,24},{9,... | collective-permute-start | bytes 147464 | tf_op jit(solution)/shard_map/ppermute | solution.py:177
  40.2 12.3 %copy-start.1 = (s32[1,32]{1,0:T(1,128)S(1)}, s32[1,32]{1,0:T(1,128)}, u32[]{:S(2)}) copy-start(s32[1,32]{1,0:T(1,128)} %param.8) | copy-start | bytes 388
  40.2 13.6 %copy-start.2 = (s32[1,128]{1,0:T(1,128)S(1)}, s32[1,128]{1,0:T(1,128)}, u32[]{:S(2)}) copy-start(s32[1,128]{1,0:T(1,128)} %param.7) | copy-start | bytes 1540
  40.2 32.5 %all-to-all-start = ((bf16[16,392,128]{2,1,0:T(8,128)(2,1)}), bf16[16,392,128]{2,1,0:T(8,128)(2,1)}, u32[]{:S(2)}, u32[]{:S(2)}) async-start(bf16[16,392,128]{2,1,0:T(8,128)(2,1)} %broadcast_in_dim.14), calls=%async_computation | async-start | bytes 3211264 | tf_op jit(solution)/shard_map/all_to_all | solution.py:199
  48.1 17.8 %collective-permute-start.2 = (bf16[32,4096]{1,0:T(8,128)(2,1)S(1)}, bf16[32,4096]{1,0:T(8,128)(2,1)S(1)}, u32[]{:S(2)}, u32[]{:S(2)}) collective-permute-start(bf16[32,4096]{1,0:T(8,128)(2,1)S(1)} %get-tuple-element.18), channel_id=1, source_target_pairs={{0,32},{32,64},{64,96},{96,128},{128,160},{160,192},{192,224},{224... | collective-permute-start | bytes 786440 | tf_op jit(solution)/shard_map/ppermute | solution.py:193
  50.1 19.3 %collective-permute-start.3 = (bf16[32,4096]{1,0:T(8,128)(2,1)S(1)}, bf16[32,4096]{1,0:T(8,128)(2,1)S(1)}, u32[]{:S(2)}, u32[]{:S(2)}) collective-permute-start(bf16[32,4096]{1,0:T(8,128)(2,1)S(1)} %get-tuple-element.17), channel_id=1, source_target_pairs={{32,0},{64,32},{96,64},{128,96},{160,128},{192,160},{224,192},{256... | collective-permute-start | bytes 786440 | tf_op jit(solution)/shard_map/ppermute | solution.py:194
  69.4 1.6 %copy-start = (bf16[1,256,4096]{2,1,0:T(8,128)(2,1)S(1)}, bf16[1,256,4096]{2,1,0:T(8,128)(2,1)}, u32[]{:S(2)}) copy-start(bf16[1,256,4096]{2,1,0:T(8,128)(2,1)} %param.5) | copy-start | bytes 6291460
  72.8 8.4 %collective-permute-start.4 = (bf16[16,392,128]{2,1,0:T(8,128)(2,1)}, bf16[16,392,128]{2,1,0:T(8,128)(2,1)S(1)}, u32[]{:S(2)}, u32[]{:S(2)}) collective-permute-start(bf16[16,392,128]{2,1,0:T(8,128)(2,1)} %all-to-all-done.half), channel_id=1, source_target_pairs={{0,32},{32,0},{1,33},{33,1},{2,34},{34,2},{3,35},{35,3},{4,36},{36... | collective-permute-start | bytes 4816904 | tf_op jit(solution)/shard_map/ppermute | solution.py:214
